TPU v7x, 32 devices: a whole 2x2x4 slice. The times are simulated.
32 devices in a mesh: groups: 2 (over y), ffn: 4 (over z), hidden: 4 (over x, core).
Axes of the slice: x: 2, y: 2, z: 4, core: 2. Of those that a mesh axis runs over, the one named last changes fastest.
Arguments:
- residual_in: bfloat16 [512, 8192], P(('groups', 'ffn'), 'hidden'), parts along dimension 0, may hold values from -10 to 10
- queries: bfloat16 [512, 8192], P(('groups', 'hidden'), 'ffn'), parts along dimension 0, may hold values from -100 to 100
- new_keys: bfloat16 [512, 1024], P(('groups', 'hidden'), 'ffn'), parts along dimension 0, may hold values from -6 to 6
- new_values: bfloat16 [512, 1024], P(('groups', 'hidden'), 'ffn'), parts along dimension 0, may hold values from -24 to 24
- key_cache: bfloat16 [32, 2048, 1024], P(('groups', 'hidden'), 'ffn'), parts along dimension 0, may hold values from -6 to 6
- value_cache: bfloat16 [32, 2048, 1024], P(('groups', 'hidden'), 'ffn'), parts along dimension 0, may hold values from -24 to 24
- cache_lengths: int32 [32], P(('groups', 'hidden')), parts along dimension 0, may hold values from 1 to 2048, as said below
- norm_gain: bfloat16 [8192], P('hidden'), may hold values from 0.099609375 to 1.8984375
- out_weight: bfloat16 [8192, 8192], P('ffn', 'hidden'), may hold values from -0.25 to 0.25
- gate_weight: bfloat16 [8192, 14336], P('hidden', 'ffn'), may hold values from -0.125 to 0.125
- up_weight: bfloat16 [8192, 14336], P('hidden', 'ffn'), may hold values from -0.125 to 0.125
- down_weight: bfloat16 [14336, 8192], P('ffn', 'hidden'), may hold values from -0.09375 to 0.09375
Outputs:
- block_out: bfloat16 [512, 8192], P(('groups', 'ffn'), 'hidden'), parts along dimension 0
There are 2 independent parts, one for each index of `groups`. A program takes and returns all parts, laid end to end along the dimension named above; an argument that names none is the same for every part. Nothing has to cross between parts.
Inputs may be any that keep to these rules, and one draw needn't show every extreme that they name: `cache_lengths`: each sequence's cached tokens fill the first cache positions; some sequence has exactly 2048.
All inputs are finite; a program needn't handle non-finite values.
Results may differ from a plain program's by a relative error of at most 0.04.
Values may be sent and summed in bfloat16 or wider, within the bound.
A program may use at most 128 MiB of HBM per device.

v0:
```python
import math

import jax
import jax.numpy as jnp
from jax import lax
from jax.sharding import PartitionSpec as P

D = 8192
HEADS = 64
KVH = 8
HD = 128
DRAFT = 16


def rope_tables(positions, head_size):
    steps_half = jnp.arange(head_size // 2).astype(jnp.float32)
    inverse = jnp.exp(steps_half * (-2.0 * math.log(500000.0) / head_size))
    angle = positions.astype(jnp.float32)[:, None] * inverse[None, :]
    return (jnp.cos(angle), jnp.sin(angle))


def rotate(values, cosine, sine_table):
    half = values.shape[-1] // 2
    first_half = values[..., :half]
    second_half = values[..., half:]
    cosine = cosine[:, None, :]
    sine_table = sine_table[:, None, :]
    return jnp.concatenate(
        [
            first_half * cosine - second_half * sine_table,
            second_half * cosine + first_half * sine_table,
        ],
        axis=-1,
    )


def shards(
    residual_in,
    queries,
    new_keys,
    new_values,
    key_cache,
    value_cache,
    cache_lengths,
    norm_gain,
    out_weight,
    gate_weight,
    up_weight,
    down_weight,
):
    group = HEADS // KVH
    seq_count = cache_lengths.shape[0]
    block = key_cache.shape[1]
    query_all, key_fresh, value_fresh = (
        lax.all_gather(queries, "ffn", axis=1, tiled=True),
        lax.all_gather(new_keys, "ffn", axis=1, tiled=True),
        lax.all_gather(new_values, "ffn", axis=1, tiled=True),
    )
    positions = (cache_lengths[:, None] + jnp.arange(DRAFT, dtype=jnp.int32)[None, :]).reshape(-1)
    cosine, sine_table = rope_tables(positions, HD)
    query_rot = rotate(
        query_all.astype(jnp.float32).reshape(-1, HEADS, HD), cosine, sine_table
    ).astype(jnp.bfloat16)
    query_rot = query_rot.reshape(seq_count, DRAFT, KVH, group, HD)
    key_rot = rotate(key_fresh.astype(jnp.float32).reshape(-1, KVH, HD), cosine, sine_table).astype(
        jnp.bfloat16
    )
    key_rot = key_rot.reshape(seq_count, DRAFT, KVH, HD)
    value_rows = value_fresh.reshape(seq_count, DRAFT, KVH, HD)
    cached_keys = key_cache.reshape(seq_count, block, KVH, HD)
    cached_values = value_cache.reshape(seq_count, block, KVH, HD)
    scaling = 1.0 / math.sqrt(HD)
    cache_scores = (
        jnp.einsum("sjkgd,spkd->sjkgp", query_rot, cached_keys, preferred_element_type=jnp.float32)
        * scaling
    )
    draft_scores = (
        jnp.einsum("sjkgd,sikd->sjkgi", query_rot, key_rot, preferred_element_type=jnp.float32)
        * scaling
    )
    ffn_index = lax.axis_index("ffn")
    slot_positions = ffn_index * block + jnp.arange(block, dtype=jnp.int32)
    usable = (slot_positions[None, :] < cache_lengths[:, None])[:, None, None, None, :]
    causal = jnp.arange(DRAFT)[None, :] <= jnp.arange(DRAFT)[:, None]
    draft_usable = jnp.logical_and(causal[None, :, None, None, :], ffn_index == 0)
    cache_scores = jnp.where(usable, cache_scores, -1e30)
    draft_scores = jnp.where(draft_usable, draft_scores, -1e30)
    local_peak = jnp.maximum(cache_scores.max(-1), draft_scores.max(-1))
    peak_score = lax.pmax(local_peak, "ffn")[..., None]
    cache_weights = jnp.where(usable, jnp.exp(cache_scores - peak_score), 0.0)
    draft_weights = jnp.where(draft_usable, jnp.exp(draft_scores - peak_score), 0.0)
    numerator = jnp.einsum(
        "sjkgp,spkd->sjkgd",
        cache_weights.astype(jnp.bfloat16),
        cached_values,
        preferred_element_type=jnp.float32,
    )
    numerator = numerator + jnp.einsum(
        "sjkgi,sikd->sjkgd",
        draft_weights.astype(jnp.bfloat16),
        value_rows,
        preferred_element_type=jnp.float32,
    )
    denominator = cache_weights.sum(-1) + draft_weights.sum(-1)
    row_count = seq_count * DRAFT
    numerator = numerator.reshape(row_count, HEADS, HD)
    denominator = denominator.reshape(row_count, HEADS)
    heads_here = out_weight.shape[0] // HD
    numerator_share, denominator_share = (
        lax.psum_scatter(
            numerator.astype(jnp.bfloat16), "ffn", scatter_dimension=1, tiled=True
        ).astype(jnp.float32),
        lax.psum_scatter(
            denominator.astype(jnp.bfloat16), "ffn", scatter_dimension=1, tiled=True
        ).astype(jnp.float32),
    )
    attended = (
        (numerator_share / denominator_share[..., None])
        .reshape(row_count, heads_here * HD)
        .astype(jnp.bfloat16)
    )
    attended_rows = lax.all_gather(attended, "hidden", axis=0, tiled=True)
    projected = lax.psum_scatter(
        jnp.dot(attended_rows, out_weight, preferred_element_type=jnp.float32).astype(jnp.bfloat16),
        "ffn",
        scatter_dimension=0,
        tiled=True,
    ).astype(jnp.float32)
    resid = (residual_in.astype(jnp.float32) + projected).astype(jnp.bfloat16)
    widened = resid.astype(jnp.float32)
    squares = lax.psum(jnp.sum(widened * widened, axis=1), "hidden")
    factor = lax.rsqrt(squares / D + 1e-05)[:, None]
    normed = (widened * factor * norm_gain.astype(jnp.float32)[None, :]).astype(jnp.bfloat16)
    units_here = gate_weight.shape[1]
    piece = lax.all_gather(normed, "ffn", axis=0, tiled=True)
    partial_inner = jnp.concatenate(
        [
            jnp.dot(piece, gate_weight, preferred_element_type=jnp.float32),
            jnp.dot(piece, up_weight, preferred_element_type=jnp.float32),
        ],
        axis=1,
    )
    summed = lax.psum(partial_inner.astype(jnp.bfloat16), "hidden").astype(jnp.float32)
    activation = (jax.nn.silu(summed[:, :units_here]) * summed[:, units_here:]).astype(jnp.bfloat16)
    lowered = lax.psum_scatter(
        jnp.dot(activation, down_weight, preferred_element_type=jnp.float32).astype(jnp.bfloat16),
        "ffn",
        scatter_dimension=0,
        tiled=True,
    ).astype(jnp.float32)
    return (widened + lowered).astype(jnp.bfloat16)


def solution(mesh):
    in_specs = (
        P(("groups", "ffn"), "hidden"),
        P(("groups", "hidden"), "ffn"),
        P(("groups", "hidden"), "ffn"),
        P(("groups", "hidden"), "ffn"),
        P(("groups", "hidden"), "ffn", None),
        P(("groups", "hidden"), "ffn", None),
        P(("groups", "hidden")),
        P("hidden"),
        P("ffn", "hidden"),
        P("hidden", "ffn"),
        P("hidden", "ffn"),
        P("ffn", "hidden"),
    )
    out_specs = P(("groups", "ffn"), "hidden")
    return jax.shard_map(shards, mesh=mesh, in_specs=in_specs, out_specs=out_specs, check_vma=False)
```

profile of v0, /device:TPU:0, one launch (start us, length us, event | category | flops | bytes accessed | tf_op | source)
XLA Modules:
  0.0 375.5 jit_solution(9837612590256703097)
XLA Ops:
  6.5 0.7 all-gather.4.cloned.1.call-update
  7.3 0.7 add_convert_fusion.5
  8.1 15.4 %all_gather.16 = bf16[64,1024]{1,0:T(8,128)(2,1)S(1)} all-gather(bf16[64,256]{1,0:T(8,128)(2,1)} %param.14), channel_id=1, replica_groups=mesh['groups'=2,'ffn'=4,'hidden'=4] {'ffn'}, dimensions={1}, use_global_device_ids=true | all-gather | bytes 163840 | tf_op jit(solution)/shard_map/all_gather | solution.py:56
  23.6 0.2 multiply_cosine_fusion
  23.8 0.2 subtract_convert_fusion.1
  24.0 15.5 %all_gather.17 = bf16[64,1024]{1,0:T(8,128)(2,1)S(1)} all-gather(bf16[64,256]{1,0:T(8,128)(2,1)} %param.15), channel_id=1, replica_groups=mesh['groups'=2,'ffn'=4,'hidden'=4] {'ffn'}, dimensions={1}, use_global_device_ids=true | all-gather | bytes 163840 | tf_op jit(solution)/shard_map/all_gather | solution.py:57
  39.5 3.5 copy.87
  43.0 1.1 copy.89
  44.3 0.7 bitcast_bitcast_fusion.2
  44.9 2.2 bitcast_bitcast_fusion.1
  47.1 2.2 bitcast_bitcast_fusion
  49.4 1.4 convert_bitcast_fusion
  50.7 0.4 copy.86
  51.1 0.9 subtract_convert_fusion
  52.0 0.6 pad_maximum_fusion.1
  52.6 2.6 fusion.16
  55.4 7.1 %bitcast_reduce_fusion = (f32[4,16,8,8]{3,1,2,0:T(8,128)S(1)}, f32[4,8,16,8,512]{4,3,2,1,0:T(8,128)}) fusion(pred[4,512]{1,0:T(4,128)(4,1)S(1)} %broadcast_compare_fusion, bf16[4,512,8,128,1]{3,2,1,0,4:T(8,128)(2,1)} %bitcast_bitcast_fusion.1, bf16[4,16,8,8,128]{4,3,2,1,0:T(8,128)(2,1)S(1)} %pad_maximum_fusion.1), kind=kOutput, calls=%fused_computation.1 | convolution fusion | flops 543158272 | bytes 13649920 | tf_op jit(solution)/shard_map/sjkgd,spkd->sjkgp/dot_general | solution.py:74
  62.5 24.8 %pmax.7 = f32[4,16,8,8]{3,1,2,0:T(8,128)S(1)} all-reduce(f32[4,16,8,8]{3,1,2,0:T(8,128)S(1)} %max.5), channel_id=1, replica_groups=mesh['groups'=2,'ffn'=4,'hidden'=4] {'ffn'}, use_global_device_ids=true, to_apply=%region_2.3 | all-reduce | flops 4096 | bytes 32768 | tf_op jit(solution)/shard_map/pmax | solution.py:89
  87.5 4.7 %fusion.2 = f32[4,16,8,8]{3,1,2,0:T(8,128)S(1)} fusion(f32[4,8,16,8,512]{4,3,2,1,0:T(8,128)} %get-tuple-element.14, f32[4,16,8,8]{3,1,2,0:T(8,128)S(1)} %pmax.7, pred[4,512]{1,0:T(4,128)(4,1)S(1)} %broadcast_compare_fusion), kind=kLoop, calls=%fused_computation.5 | loop fusion | flops 10481664 | bytes 8423424 | tf_op jit(solution)/shard_map/reduce_sum | solution.py:104
  92.2 0.8 copy.71
  93.0 1.0 fusion.19
  93.9 0.9 add_convert_fusion.4
  94.9 0.7 convert_element_type.104
  95.7 0.8 copy.68
  96.5 7.0 %fusion.4 = f32[4,8,16,8,128]{4,3,2,1,0:T(8,128)S(1)} fusion(f32[4,8,16,8,512]{4,3,2,1,0:T(8,128)} %get-tuple-element.14, bf16[4,512,8,128,1]{3,2,1,0,4:T(8,128)(2,1)} %bitcast_bitcast_fusion, f32[4,16,8,8]{3,1,2,0:T(8,128)S(1)} %pmax.7, pred[4,512]{1,0:T(4,128)(4,1)S(1)} %broadcast_compare_fusion), kind=kOutput, calls=%fused_computation.9 | convolution fusion | flops 547356672 | bytes 14698496 | tf_op jit(solution)/shard_map/sjkgp,spkd->sjkgd/dot_general | solution.py:92
  103.5 0.4 fusion.21
  104.0 1.3 copy.70
  105.3 8.2 %reduce-scatter.7.cloned.1.call-done = bf16[64,16]{0,1:T(8,128)(2,1)} async-done(((bf16[64,64]{0,1:T(8,128)(2,1)}), bf16[64,16]{0,1:T(8,128)(2,1)}) %reduce-scatter.7.cloned.1.call-update) | async-done | bytes 2064 | tf_op jit(solution)/shard_map/reduce_scatter | solution.py:113
  113.5 0.8 copy.73
  114.3 27.0 %reduce-scatter.5.cloned.1.call-done = bf16[64,16,128]{2,1,0:T(8,128)(2,1)} async-done(((bf16[64,64,128]{2,1,0:T(8,128)(2,1)}), bf16[64,16,128]{2,1,0:T(8,128)(2,1)}) %reduce-scatter.5.cloned.1.call-update) | async-done | bytes 262160 | tf_op jit(solution)/shard_map/reduce_scatter | solution.py:110
  141.3 1.2 divide_convert_fusion
  142.5 0.8 copy.109
  143.3 15.3 %all-gather.6.cloned.1.call-done = bf16[256,2048]{1,0:T(8,128)(2,1)} async-done(((bf16[64,2048]{1,0:T(8,128)(2,1)}), bf16[256,2048]{1,0:T(8,128)(2,1)}) %all-gather.6.cloned.1.call-update) | async-done | bytes 1048592 | tf_op jit(solution)/shard_map/all_gather | solution.py:122
  158.6 7.0 %convolution_convert_fusion.3 = bf16[256,2048]{1,0:T(8,128)(2,1)} fusion(bf16[256,2048]{1,0:T(8,128)(2,1)} %all-gather.6.cloned.1.call-done, bf16[2048,2048]{1,0:T(8,128)(2,1)} %param.20), kind=kOutput, calls=%fused_computation.25 | convolution fusion | flops 2148007936 | bytes 10485760 | tf_op jit(solution)/shard_map/dot_general | solution.py:124
  165.7 27.4 %reduce-scatter.9.cloned.1.call-done = bf16[64,2048]{1,0:T(8,128)(2,1)} async-done(((bf16[256,2048]{1,0:T(8,128)(2,1)}), bf16[64,2048]{1,0:T(8,128)(2,1)}) %reduce-scatter.9.cloned.1.call-update) | async-done | bytes 262160 | tf_op jit(solution)/shard_map/reduce_scatter | solution.py:123
  193.1 1.1 fusion.25
  194.2 6.2 %psum.14 = f32[64]{0:T(128)S(1)} all-reduce(f32[64]{0:T(128)S(1)} %fusion.25), channel_id=1, replica_groups=mesh['groups'=2,'ffn'=4,'hidden'=4] {'hidden'}, use_global_device_ids=true, to_apply=%region_9.10 | all-reduce | flops 64 | bytes 512 | tf_op jit(solution)/shard_map/psum | solution.py:131
  200.4 1.8 fusion.27
  202.2 0.3 all-reduce.2.cloned.1.call-start
  202.5 26.1 %all-gather.8.cloned.1.call-done = bf16[256,2048]{1,0:T(8,128)(2,1)} async-done(((bf16[64,2048]{1,0:T(8,128)(2,1)}), bf16[256,2048]{1,0:T(8,128)(2,1)}) %all-gather.8.cloned.1.call-update) | async-done | bytes 1048592 | tf_op jit(solution)/shard_map/all_gather | solution.py:135
  228.6 9.5 %convolution_convert_fusion = bf16[256,3584]{1,0:T(8,128)(2,1)S(1)} fusion(bf16[256,2048]{1,0:T(8,128)(2,1)} %all-gather.8.cloned.1.call-done, bf16[2048,3584]{1,0:T(8,128)(2,1)} %param.22), kind=kOutput, calls=%fused_computation.7 | convolution fusion | flops 3759013888 | bytes 17563648 | tf_op jit(solution)/shard_map/dot_general | solution.py:139
  238.2 9.1 %convolution_convert_fusion.1 = bf16[256,3584]{1,0:T(8,128)(2,1)S(1)} fusion(bf16[256,2048]{1,0:T(8,128)(2,1)S(1)} %copy-done.6, bf16[2048,3584]{1,0:T(8,128)(2,1)} %param.21), kind=kOutput, calls=%fused_computation.8 | convolution fusion | flops 3759013888 | bytes 17563648 | tf_op jit(solution)/shard_map/dot_general | solution.py:138
  247.3 2.3 pad_maximum_fusion
  249.6 76.5 %all-reduce.2.cloned.1.call-done = bf16[256,7168]{1,0:T(8,128)(2,1)} async-done(((bf16[256,7168]{1,0:T(8,128)(2,1)}), bf16[256,7168]{1,0:T(8,128)(2,1)}) %all-reduce.2.cloned.1.call-update) | async-done | bytes 3670032 | tf_op jit(solution)/shard_map/psum | solution.py:143
  326.1 2.9 convert_element_type.114
  329.0 10.3 %convolution_convert_fusion.2 = bf16[256,2048]{1,0:T(8,128)(2,1)} fusion(bf16[3584,2048]{1,0:T(8,128)(2,1)} %param.23, f32[256,7168]{1,0:T(8,128)S(1)} %convert_element_type.114), kind=kOutput, calls=%fused_computation.24 | convolution fusion | flops 3764125696 | bytes 23068672 | tf_op jit(solution)/shard_map/dot_general | solution.py:146
  339.3 27.6 %reduce-scatter.11.cloned.1.call-done = bf16[64,2048]{1,0:T(8,128)(2,1)} async-done(((bf16[256,2048]{1,0:T(8,128)(2,1)}), bf16[64,2048]{1,0:T(8,128)(2,1)}) %reduce-scatter.11.cloned.1.call-update) | async-done | bytes 262160 | tf_op jit(solution)/shard_map/reduce_scatter | solution.py:145
  366.9 1.7 fusion.28
  (45 shorter events, 1.1 us)
Async XLA Ops:
  6.5 42.8 %all-gather.4.cloned.1.call-start = ((), (), s32[]{:S(2)}) async-start(), calls=%async_computation.4 | async-start | bytes 1310720 | tf_op jit(solution)/shard_map/all_gather | solution.py:55
  7.3 106.3 %reduce-scatter.7.cloned.1.call-start = ((), (), s32[]{:S(2)}) async-start(), calls=%async_computation.6 | async-start | bytes 20480 | tf_op jit(solution)/shard_map/reduce_scatter | solution.py:113
  39.5 3.5 copy-start
  43.0 1.2 copy-start.5
  95.6 45.7 %reduce-scatter.5.cloned.1.call-start = ((), (), s32[]{:S(2)}) async-start(), calls=%async_computation.5 | async-start | bytes 1310720 | tf_op jit(solution)/shard_map/reduce_scatter | solution.py:110
  96.5 7.0 %copy-start.3 = (bf16[4,16,8,128,1]{3,2,1,0,4:T(8,128)(2,1)S(1)}, bf16[4,16,8,128,1]{3,2,1,0,4:T(8,128)(2,1)}, u32[]{:S(2)}) copy-start(bf16[4,16,8,128,1]{3,2,1,0,4:T(8,128)(2,1)} %bitcast_bitcast_fusion.2) | copy-start | bytes 393220
  105.2 53.4 %all-gather.6.cloned.1.call-start = ((), (), s32[]{:S(2)}) async-start(), calls=%async_computation.7 | async-start | bytes 1310720 | tf_op jit(solution)/shard_map/all_gather | solution.py:122
  143.3 22.4 %copy-start.4 = (bf16[2048]{0:T(1024)(128)(2,1)S(1)}, bf16[2048]{0:T(1024)(128)(2,1)}, u32[]{:S(2)}) copy-start(bf16[2048]{0:T(1024)(128)(2,1)} %param.19) | copy-start | bytes 12292
  143.3 49.8 %copy-start.1 = (bf16[64,2048]{1,0:T(8,128)(2,1)S(1)}, bf16[64,2048]{1,0:T(8,128)(2,1)}, u32[]{:S(2)}) copy-start(bf16[64,2048]{1,0:T(8,128)(2,1)} %param.12) | copy-start | bytes 786436
  143.3 49.8 %reduce-scatter.9.cloned.1.call-start = ((), (), s32[]{:S(2)}) async-start(), calls=%async_computation.8 | async-start | bytes 1310720 | tf_op jit(solution)/shard_map/reduce_scatter | solution.py:123
  165.7 63.0 %all-gather.8.cloned.1.call-start = ((), (), s32[]{:S(2)}) async-start(), calls=%async_computation.9 | async-start | bytes 1310720 | tf_op jit(solution)/shard_map/all_gather | solution.py:135
  202.2 123.9 %all-reduce.2.cloned.1.call-start = ((), (), s32[]{:S(2)}) async-start(), calls=%async_computation.10 | async-start | bytes 7340032 | tf_op jit(solution)/shard_map/psum | solution.py:143
  228.6 9.5 %copy-start.6 = (bf16[256,2048]{1,0:T(8,128)(2,1)S(1)}, bf16[256,2048]{1,0:T(8,128)(2,1)}, u32[]{:S(2)}) copy-start(bf16[256,2048]{1,0:T(8,128)(2,1)} %all-gather.8.cloned.1.call-done) | copy-start | bytes 3145732
  249.6 117.3 %reduce-scatter.11.cloned.1.call-start = ((), (), s32[]{:S(2)}) async-start(), calls=%async_computation.11 | async-start | bytes 1310720 | tf_op jit(solution)/shard_map/reduce_scatter | solution.py:145
  329.0 37.9 %copy-start.2 = (bf16[64,2048]{1,0:T(8,128)(2,1)S(1)}, bf16[64,2048]{1,0:T(8,128)(2,1)}, u32[]{:S(2)}) copy-start(bf16[64,2048]{1,0:T(8,128)(2,1)} %reduce-scatter.9.cloned.1.call-done) | copy-start | bytes 786436
Sparse Core Ops, SparseCore 0:
  8.9 33.5 all-gather.3
  95.8 17.7 reduce-scatter.6
  115.8 25.4 reduce-scatter.4
  143.4 15.1 all-gather.5
  165.8 27.2 reduce-scatter.8
  202.3 26.2 all-gather.7
  249.7 76.3 all-reduce.1
  339.4 27.4 reduce-scatter.10
where the time goes:
time: 376 us; the launch traced here: 375 us
  waiting for transfers between devices  209 us (56%)
  blocking collectives  61.9 us (16%)
  matrix products  53.1 us (14%)
  other arithmetic  21.6 us (6%)
  local copies, waits for them, and re-layouts  15.6 us (4%)
  between operations  13.8 us (4%)
    psum x1, waiting for transfers between devices, shards(): lax.psum(partial_inner.astype(jnp.bfloat16), 'hidden').astype(jnp.float32)  76.5 us
    reduce_scatter x1, waiting for transfers between devices, shards(): lax.psum_scatter(jnp.dot(activation, down_weight, preferred_element_type=...  27.6 us
    reduce_scatter x1, waiting for transfers between devices, shards(): lax.psum_scatter(jnp.dot(attended_rows, out_weight, preferred_element_typ...  27.4 us
    reduce_scatter x1, waiting for transfers between devices, shards(): lax.psum_scatter(numerator.astype(jnp.bfloat16), 'ffn', scatter_dimension...  27 us
    all_gather x1, waiting for transfers between devices, shards(): piece = lax.all_gather(normed, 'ffn', axis=0, tiled=True)  26.1 us
    pmax x1, blocking collectives, shards(): peak_score = lax.pmax(local_peak, 'ffn')[..., None]  24.8 us
    all_gather x1, blocking collectives, shards(): lax.all_gather(new_values, 'ffn', axis=1, tiled=True)  15.5 us
    all_gather x1, blocking collectives, shards(): lax.all_gather(new_keys, 'ffn', axis=1, tiled=True)  15.4 us
  transfers between devices with their start and end apart: 8, of which 7 were waited for; matrix products, arithmetic and copies ran while one was open for 6% of the time, Pallas kernels for 0%

commit v1 on v0

v1 whole, which is shorter than its diff:
```python
import functools
import math

import jax
import jax.numpy as jnp
from jax import lax
from jax.experimental import pallas as pl
from jax.experimental.pallas import tpu as pltpu
from jax.sharding import PartitionSpec as P

D = 8192
HEADS = 64
KVH = 8
HD = 128
DRAFT = 16
GROUP = HEADS // KVH
F32 = jnp.float32
BF16 = jnp.bfloat16
MESH = pl.DeviceIdType.MESH
SLOTS = 3


def kernel(
    cfg,
    cos_ref,
    sin_ref,
    bias_ref,
    dbias_ref,
    q_ref,
    k_ref,
    v_ref,
    resin_ref,
    gain_ref,
    kc_hbm,
    vc_hbm,
    ow_hbm,
    gw_hbm,
    uw_hbm,
    dw_hbm,
    out_ref,
    kbuf,
    vbuf,
    ow,
    gbuf,
    ubuf,
    dw,
    qall,
    kall,
    vall,
    num_send,
    num_recv,
    lse_send,
    lse_recv,
    att,
    pp,
    pp_recv,
    resid,
    sq,
    sq_recv,
    nrm,
    part,
    r1,
    s2,
    s2_recv,
    act,
    acc,
    dn_recv,
    kv_sem,
    w_sem,
    gu_sem,
    qkv_ss,
    qkv_rs,
    num_ss,
    num_rs,
    att_ss,
    att_rs,
    pp_ss,
    pp_rs,
    sq_ss,
    sq_rs,
    nrm_ss,
    nrm_rs,
    r1_ss,
    r1_rs,
    s2_ss,
    s2_rs,
    act_ss,
    act_rs,
    dn_ss,
    dn_rs,
):
    nf, nh, seqs, tile, tiles = cfg
    nx = nh // 2
    me_f = lax.axis_index("ffn")
    me_h = lax.axis_index("hidden")
    core = lax.rem(me_h, 2)
    me_x = me_h // 2
    partner = me_x * 2 + (1 - core)
    rows = q_ref.shape[0]
    rr = resin_ref.shape[0]
    width = resin_ref.shape[1]
    hh = q_ref.shape[1] // HD

    def fpeer(d):
        return lax.rem(me_f + d, nf)

    def ffrom(d):
        return lax.rem(me_f + nf - d, nf)

    def hpeer(d):
        return lax.rem(me_h + d, nh)

    def xpeer(d):
        return lax.rem(me_x + d, nx) * 2 + core

    def xfrom(d):
        return lax.rem(me_x + nx - d, nx)

    def fcopy(src, dst, ss, rs, dev):
        return pltpu.make_async_remote_copy(
            src_ref=src, dst_ref=dst, send_sem=ss, recv_sem=rs,
            device_id={"ffn": dev}, device_id_type=MESH,
        )

    def hcopy(src, dst, ss, rs, dev):
        return pltpu.make_async_remote_copy(
            src_ref=src, dst_ref=dst, send_sem=ss, recv_sem=rs,
            device_id={"hidden": dev}, device_id_type=MESH,
        )

    def kv_copies(s):
        slot = lax.rem(s, 2)
        return (
            pltpu.make_async_copy(kc_hbm.at[s], kbuf.at[slot], kv_sem.at[0, slot]),
            pltpu.make_async_copy(vc_hbm.at[s], vbuf.at[slot], kv_sem.at[1, slot]),
        )

    def gu_copies(t):
        slot = lax.rem(t, SLOTS)
        if tiles == 1:
            cols = pl.ds(0, tile)
        else:
            cols = pl.ds(pl.multiple_of(t * tile, tile), tile)
        return (
            pltpu.make_async_copy(gw_hbm.at[:, cols], gbuf.at[slot], gu_sem.at[0, slot]),
            pltpu.make_async_copy(uw_hbm.at[:, cols], ubuf.at[slot], gu_sem.at[1, slot]),
        )

    ow_copy = pltpu.make_async_copy(ow_hbm, ow, w_sem.at[0])
    dw_copy = pltpu.make_async_copy(dw_hbm, dw, w_sem.at[1])

    for s in range(min(2, seqs)):
        for c in kv_copies(s):
            c.start()

    barrier = pltpu.get_barrier_semaphore()
    for d in range(1, nf):
        pl.semaphore_signal(barrier, inc=1, device_id={"ffn": fpeer(d)}, device_id_type=MESH)
    for d in range(1, nh):
        pl.semaphore_signal(barrier, inc=1, device_id={"hidden": hpeer(d)}, device_id_type=MESH)

    cos = cos_ref[...]
    sin = sin_ref[...]

    for h in range(hh):
        x = q_ref[:, h * HD : (h + 1) * HD].astype(F32)
        qall[me_f, :, h * HD : (h + 1) * HD] = (
            x * cos + pltpu.roll(x, HD // 2, 1) * sin
        ).astype(BF16)
    kall[me_f] = k_ref[...]
    vall[me_f] = v_ref[...]

    pl.semaphore_wait(barrier, nf - 1 + nh - 1)

    def qkv(d):
        return [
            fcopy(buf.at[me_f], buf.at[me_f], qkv_ss.at[i, d], qkv_rs.at[i, d], fpeer(d))
            for i, buf in enumerate((qall, kall, vall))
        ]

    for d in range(1, nf):
        for c in qkv(d):
            c.start()
    ow_copy.start()
    for d in range(1, nf):
        for c in qkv(d):
            c.wait_recv()

    kw = k_ref.shape[1]

    def kv_head(buf, k, r0):
        if kw >= HD:
            per = kw // HD
            lo = (k % per) * HD
            return buf[k // per, pl.ds(r0, DRAFT), lo : lo + HD]
        per = HD // kw
        return jnp.concatenate(
            [buf[k * per + i, pl.ds(r0, DRAFT), :] for i in range(per)], axis=1
        )

    scaling = 1.0 / math.sqrt(HD)
    nt = (((1,), (1,)), ((), ()))

    def attend(s, carry):
        slot = lax.rem(s, 2)
        for c in kv_copies(s):
            c.wait()
        r0 = pl.multiple_of(s * DRAFT, DRAFT)
        cs = cos_ref[pl.ds(r0, DRAFT), :]
        sn = sin_ref[pl.ds(r0, DRAFT), :]
        bias = bias_ref[s]
        dbias = dbias_ref[...]
        for k in range(KVH):
            pieces = []
            for g in range(GROUP):
                h = k * GROUP + g
                lo = (h % hh) * HD
                pieces.append(qall[h // hh, pl.ds(r0, DRAFT), lo : lo + HD])
            q = jnp.concatenate(pieces, axis=0)
            keys = kbuf[slot, :, k * HD : (k + 1) * HD]
            values = vbuf[slot, :, k * HD : (k + 1) * HD]
            kd = kv_head(kall, k, r0).astype(F32)
            kd = (kd * cs + pltpu.roll(kd, HD // 2, 1) * sn).astype(BF16)
            vd = kv_head(vall, k, r0)
            sc = lax.dot_general(q, keys, nt, preferred_element_type=F32) * scaling + bias
            sd = lax.dot_general(q, kd, nt, preferred_element_type=F32) * scaling + dbias
            m = jnp.maximum(
                jnp.max(sc, axis=1, keepdims=True), jnp.max(sd, axis=1, keepdims=True)
            )
            w = jnp.exp(sc - m)
            wd = jnp.exp(sd - m)
            total = jnp.sum(w, axis=1, keepdims=True) + jnp.sum(wd, axis=1, keepdims=True)
            num = jnp.dot(w.astype(BF16), values, preferred_element_type=F32)
            num = num + jnp.dot(wd.astype(BF16), vd, preferred_element_type=F32)
            o = (num / total).astype(BF16)
            lse = m + jnp.log(total)
            for g in range(GROUP):
                h = k * GROUP + g
                lo = (h % hh) * HD
                num_send[h // hh, pl.ds(r0, DRAFT), lo : lo + HD] = o[
                    g * DRAFT : (g + 1) * DRAFT
                ]
                lse_send[h // hh, pl.ds(r0, DRAFT), h % hh : h % hh + 1] = lse[
                    g * DRAFT : (g + 1) * DRAFT
                ]

        @pl.when(s + 2 < seqs)
        def _():
            for c in kv_copies(s + 2):
                c.start()

        return carry

    lax.fori_loop(0, seqs, attend, 0)

    def nums(d):
        p = fpeer(d)
        return [
            fcopy(num_send.at[p], num_recv.at[d - 1], num_ss.at[0, d], num_rs.at[0, d], p),
            fcopy(lse_send.at[p], lse_recv.at[d - 1], num_ss.at[1, d], num_rs.at[1, d], p),
        ]

    for d in range(1, nf):
        for c in nums(d):
            c.start()
    for t in range(min(SLOTS, tiles)):
        for c in gu_copies(t):
            c.start()
    dw_copy.start()
    for d in range(1, nf):
        for c in nums(d):
            c.wait_recv()
    for h in range(hh):
        lo = h * HD
        ls = [lse_send[me_f, :, h : h + 1]] + [
            lse_recv[d - 1, :, h : h + 1] for d in range(1, nf)
        ]
        ns = [num_send[me_f, :, lo : lo + HD]] + [
            num_recv[d - 1, :, lo : lo + HD] for d in range(1, nf)
        ]
        top = functools.reduce(jnp.maximum, ls)
        ws = [jnp.exp(x - top) for x in ls]
        tot = functools.reduce(jnp.add, ws)
        val = functools.reduce(jnp.add, [w * n.astype(F32) for w, n in zip(ws, ns)])
        att[me_h, :, lo : lo + HD] = (val / tot).astype(BF16)

    def att_x(d):
        return hcopy(att.at[me_h], att.at[me_h], att_ss.at[d], att_rs.at[d], xpeer(d))

    def att_p(d):
        b = xfrom(d) * 2 + core
        return hcopy(att.at[b], att.at[b], att_ss.at[nx + d], att_rs.at[nx + d], partner)

    for d in range(1, nx):
        att_x(d).start()
    att_p(0).start()
    for d in range(1, nx):
        att_x(d).wait_recv()
        att_p(d).start()
    for d in range(nx):
        att_p(d).wait_recv()

    ow_copy.wait()
    step = width if width % 512 else 512
    total_rows = nh * rows

    def project(i, carry):
        cols = pl.ds(pl.multiple_of(i * step, step), step) if width != step else slice(None)
        x = att[...].reshape(total_rows, att.shape[2])
        pp[:, cols] = jnp.dot(x, ow[:, cols], preferred_element_type=F32).astype(BF16)
        return carry

    lax.fori_loop(0, width // step, project, 0)

    def own_rows(p):
        return pl.ds(pl.multiple_of(p * rr, rr), rr)

    def pps(d):
        p = fpeer(d)
        return fcopy(pp.at[own_rows(p)], pp_recv.at[d - 1], pp_ss.at[d], pp_rs.at[d], p)

    for d in range(1, nf):
        pps(d).start()
    for d in range(1, nf):
        pps(d).wait_recv()
    x = pp[own_rows(me_f), :].astype(F32)
    for d in range(1, nf):
        x = x + pp_recv[d - 1].astype(F32)
    x = (resin_ref[...].astype(F32) + x).astype(BF16).astype(F32)
    resid[...] = x
    mine = jnp.sum(x * x, axis=1, keepdims=True)
    sq[...] = jnp.broadcast_to(mine, sq.shape)

    def sqs(d):
        return hcopy(sq, sq_recv.at[d - 1], sq_ss.at[d], sq_rs.at[d], hpeer(d))

    for d in range(1, nh):
        sqs(d).start()
    for d in range(1, nh):
        sqs(d).wait_recv()
    squares = mine
    for d in range(1, nh):
        squares = squares + sq_recv[d - 1, :, 0:1]
    factor = lax.rsqrt(squares / D + 1e-05)
    nrm[me_f] = (resid[...] * factor * gain_ref[...].astype(F32)).astype(BF16)

    def nrms(d):
        return fcopy(nrm.at[me_f], nrm.at[me_f], nrm_ss.at[d], nrm_rs.at[d], fpeer(d))

    for d in range(1, nf):
        nrms(d).start()
    acc[...] = jnp.zeros_like(acc)
    dw_copy.wait()
    for d in range(1, nf):
        nrms(d).wait_recv()

    qr = total_rows // nh

    def r1_copy(t):
        return hcopy(part.at[t, 1 - core], r1.at[t], r1_ss.at[t], r1_rs.at[t], partner)

    def s2_copy(t, d):
        return hcopy(
            s2.at[t, d - 1], s2_recv.at[t, d - 1], s2_ss.at[t, d], s2_rs.at[t, d], xpeer(d)
        )

    def act_x(t, d):
        a = act.at[t, me_h]
        return hcopy(a, a, act_ss.at[t, d], act_rs.at[t, d], xpeer(d))

    def act_p(t, d):
        a = act.at[t, xfrom(d) * 2 + core]
        return hcopy(a, a, act_ss.at[t, nx + d], act_rs.at[t, nx + d], partner)

    def inner(t, carry):
        @pl.when(t < tiles)
        def _():
            slot = lax.rem(t, SLOTS)
            for c in gu_copies(t):
                c.wait()
            x = nrm[...].reshape(total_rows, width)
            for i, buf in enumerate((gbuf, ubuf)):
                y = jnp.dot(x, buf[slot], preferred_element_type=F32).astype(BF16)
                for b in range(nh):
                    part[t, b % 2, b // 2, i] = y[b * qr : (b + 1) * qr]
            r1_copy(t).start()

            @pl.when(t + SLOTS < tiles)
            def _():
                for c in gu_copies(t + SLOTS):
                    c.start()

        @pl.when(jnp.logical_and(t >= 1, t < tiles + 1))
        def _():
            u = t - 1
            r1_copy(u).wait_recv()
            for d in range(1, nx):
                o = lax.rem(me_x + d, nx)
                s2[u, d - 1] = (
                    part[u, core, o].astype(F32) + r1[u, o].astype(F32)
                ).astype(BF16)
                s2_copy(u, d).start()

        @pl.when(jnp.logical_and(t >= 2, t < tiles + 2))
        def _():
            u = t - 2
            for d in range(1, nx):
                s2_copy(u, d).wait_recv()
            y = part[u, core, me_x].astype(F32) + r1[u, me_x].astype(F32)
            for d in range(1, nx):
                y = y + s2_recv[u, d - 1].astype(F32)
            gate = y[0]
            up = y[1]
            act[u, me_h] = (gate / (1.0 + jnp.exp(-gate)) * up).astype(BF16)
            for d in range(1, nx):
                act_x(u, d).start()
            act_p(u, 0).start()

        @pl.when(jnp.logical_and(t >= 3, t < tiles + 3))
        def _():
            u = t - 3
            for d in range(1, nx):
                act_x(u, d).wait_recv()
                act_p(u, d).start()

        @pl.when(t >= 4)
        def _():
            u = t - 4
            for d in range(nx):
                act_p(u, d).wait_recv()
            x = act[u].reshape(total_rows, tile)
            k0 = pl.multiple_of(u * tile, tile)

            def down(i, c):
                cols = pl.ds(pl.multiple_of(i * step, step), step) if width != step else slice(None)
                acc[:, cols] += jnp.dot(x, dw[pl.ds(k0, tile), cols], preferred_element_type=F32)
                return c

            lax.fori_loop(0, width // step, down, 0)

        return carry

    lax.fori_loop(0, tiles + 4, inner, 0)

    for d in range(1, nf):
        pps(d).wait_send()
    pp[...] = acc[...].astype(BF16)

    def dns(d):
        p = fpeer(d)
        return fcopy(pp.at[own_rows(p)], dn_recv.at[d - 1], dn_ss.at[d], dn_rs.at[d], p)

    for d in range(1, nf):
        dns(d).start()
    for d in range(1, nf):
        dns(d).wait_recv()
    y = pp[own_rows(me_f), :].astype(F32)
    for d in range(1, nf):
        y = y + dn_recv[d - 1].astype(F32)
    out_ref[...] = (resid[...] + y).astype(BF16)

    for d in range(1, nf):
        for c in qkv(d) + nums(d):
            c.wait_send()
        nrms(d).wait_send()
        dns(d).wait_send()
    for d in range(1, nh):
        sqs(d).wait_send()
    for d in range(1, nx):
        att_x(d).wait_send()
    for d in range(nx):
        att_p(d).wait_send()

    def drain(t, carry):
        r1_copy(t).wait_send()
        for d in range(1, nx):
            s2_copy(t, d).wait_send()
            act_x(t, d).wait_send()
        for d in range(nx):
            act_p(t, d).wait_send()
        return carry

    lax.fori_loop(0, tiles, drain, 0)


def solution(mesh):
    nf = mesh.shape["ffn"]
    nh = mesh.shape["hidden"]
    nx = nh // 2

    def shards(
        residual_in, queries, new_keys, new_values, key_cache, value_cache,
        cache_lengths, norm_gain, out_weight, gate_weight, up_weight, down_weight,
    ):
        seqs, block, kvw = key_cache.shape
        rows, qw = queries.shape
        kw = new_keys.shape[1]
        rr, width = residual_in.shape
        units = gate_weight.shape[1]
        hh = qw // HD
        tile = 512 if units % 512 == 0 else units
        tiles = units // tile
        total_rows = rows * nh
        qr = total_rows // nh

        positions = cache_lengths[:, None] + jnp.arange(DRAFT, dtype=jnp.int32)[None, :]
        steps_half = jnp.arange(HD // 2).astype(F32)
        inverse = jnp.exp(steps_half * (-2.0 * math.log(500000.0) / HD))
        angle = positions.reshape(-1).astype(F32)[:, None] * inverse[None, :]
        cos, sin = jnp.cos(angle), jnp.sin(angle)
        cos = jnp.concatenate([cos, cos], axis=1)
        sin = jnp.concatenate([-sin, sin], axis=1)
        ffn = lax.axis_index("ffn")
        slots = ffn * block + jnp.arange(block, dtype=jnp.int32)
        bias = jnp.where(slots[None, :] < cache_lengths[:, None], 0.0, -1e30).astype(F32)
        bias = bias[:, None, :]
        token = jnp.arange(GROUP * DRAFT, dtype=jnp.int32) % DRAFT
        causal = jnp.arange(DRAFT, dtype=jnp.int32)[None, :] <= token[:, None]
        dbias = jnp.where(jnp.logical_and(causal, ffn == 0), 0.0, -1e30).astype(F32)

        vm = pl.BlockSpec(memory_space=pltpu.VMEM)
        hbm = pl.BlockSpec(memory_space=pl.ANY)
        dma = pltpu.SemaphoreType.DMA
        V = pltpu.VMEM
        scratch = [
            V((2, block, kvw), BF16),
            V((2, block, kvw), BF16),
            V(out_weight.shape, BF16),
            V((SLOTS, width, tile), BF16),
            V((SLOTS, width, tile), BF16),
            V(down_weight.shape, BF16),
            V((nf, rows, qw), BF16),
            V((nf, rows, kw), BF16),
            V((nf, rows, kw), BF16),
            V((nf, rows, qw), BF16),
            V((nf - 1, rows, qw), BF16),
            V((nf, rows, hh), F32),
            V((nf - 1, rows, hh), F32),
            V((nh, rows, qw), BF16),
            V((total_rows, width), BF16),
            V((nf - 1, rr, width), BF16),
            V((rr, width), F32),
            V((rr, HD), F32),
            V((nh - 1, rr, HD), F32),
            V((nf, rr, width), BF16),
            V((tiles, 2, nx, 2, qr, tile), BF16),
            V((tiles, nx, 2, qr, tile), BF16),
            V((tiles, nx - 1, 2, qr, tile), BF16),
            V((tiles, nx - 1, 2, qr, tile), BF16),
            V((tiles, nh, qr, tile), BF16),
            V((total_rows, width), F32),
            V((nf - 1, rr, width), BF16),
            dma((2, 2)),
            dma((2,)),
            dma((2, SLOTS)),
            dma((3, nf)), dma((3, nf)),
            dma((2, nf)), dma((2, nf)),
            dma((2 * nx,)), dma((2 * nx,)),
            dma((nf,)), dma((nf,)),
            dma((nh,)), dma((nh,)),
            dma((nf,)), dma((nf,)),
            dma((tiles,)), dma((tiles,)),
            dma((tiles, nx)), dma((tiles, nx)),
            dma((tiles, 2 * nx)), dma((tiles, 2 * nx)),
            dma((nf,)), dma((nf,)),
        ]
        return pl.pallas_call(
            functools.partial(kernel, (nf, nh, seqs, tile, tiles)),
            out_shape=jax.ShapeDtypeStruct((rr, width), BF16),
            in_specs=[vm] * 9 + [hbm] * 6,
            out_specs=vm,
            scratch_shapes=scratch,
            compiler_params=pltpu.CompilerParams(
                collective_id=0, has_side_effects=True, vmem_limit_bytes=67043328
            ),
        )(
            cos, sin, bias, dbias, queries, new_keys, new_values, residual_in,
            norm_gain[None, :], key_cache, value_cache, out_weight, gate_weight,
            up_weight, down_weight,
        )

    in_specs = (
        P(("groups", "ffn"), "hidden"),
        P(("groups", "hidden"), "ffn"),
        P(("groups", "hidden"), "ffn"),
        P(("groups", "hidden"), "ffn"),
        P(("groups", "hidden"), "ffn", None),
        P(("groups", "hidden"), "ffn", None),
        P(("groups", "hidden")),
        P("hidden"),
        P("ffn", "hidden"),
        P("hidden", "ffn"),
        P("hidden", "ffn"),
        P("ffn", "hidden"),
    )
    out_specs = P(("groups", "ffn"), "hidden")
    return jax.shard_map(shards, mesh=mesh, in_specs=in_specs, out_specs=out_specs, check_vma=False)
```

time: 376 us -> 199 us (0.53)
  the two profiles are of different devices: /device:TPU:0 before, /device:TPU:24 now
where the time goes in v1:
time: 199 us
  Pallas kernels  192 us (96%)
  other arithmetic  3.69 us (2%)
  local copies, waits for them, and re-layouts  3.04 us (2%)
    pallas_call x1, Pallas kernels, shards(): pl.pallas_call(functools.partial(kernel, (nf, nh, seqs, tile, tiles)), ou...  192 us

profile of v1, /device:TPU:24, one launch (start us, length us, event | category | flops | bytes accessed | tf_op | source)
XLA Modules:
  0.0 198.5 jit_solution(3703116469690781765)
XLA Ops:
  0.0 0.7 add_convert_fusion
  0.8 0.1 convert_element_type.18
  0.8 1.3 compare_select_fusion.bias_ref
  2.2 1.3 broadcast_in_dim.32.gain_ref
  3.4 0.7 fusion.1.dbias_ref
  4.2 0.2 fusion.2
  4.4 0.7 pad_maximum_fusion
  5.1 191.7 %shard_map.118 = bf16[64,2048]{1,0:T(8,128)(2,1)} custom-call(f32[64,128]{1,0:T(8,128)} %get-tuple-element.8.cos_ref, f32[64,128]{1,0:T(8,128)} %get-tuple-element.9.sin_ref, f32[4,1,512]{2,1,0:T(1,128)} %compare_select_fusion.bias_ref, f32[128,16]{1,0:T(8,128)} %fusion.1.dbias_ref, bf16[64,2048]{1,0:T(8,128)(2,1)} %q_ref.1, bf16[64,256]{1,0:T(8,128)(2,1)} %k_ref.1, ...), custom_call_target="tpu_custom_call" | custom-call | tf_op jit(solution)/shard_map/pallas_call | solution.py:567
  196.8 1.7 copy.14
  (3 shorter events, 0.0 us)

commit v2 on v1

--- a/solution.py
+++ b/solution.py
@@ -65,6 +65,7 @@
     act,
     acc,
     dn_recv,
+    low,
     kv_sem,
     w_sem,
     gu_sem,
@@ -128,6 +129,107 @@
             device_id={"hidden": dev}, device_id_type=MESH,
         )
 
+    has_left = me_f > 0
+    has_right = me_f < nf - 1
+
+    def g_copy(buf, ss, rs, i, right, b):
+        return fcopy(
+            buf.at[b], buf.at[b], ss.at[i, right, b], rs.at[i, b],
+            me_f + 1 if right else me_f - 1,
+        )
+
+    def chain_start(bufs, ss, rs):
+        for i, buf in enumerate(bufs):
+
+            @pl.when(has_right)
+            def _():
+                g_copy(buf, ss, rs, i, 1, me_f).start()
+
+            @pl.when(has_left)
+            def _():
+                g_copy(buf, ss, rs, i, 0, me_f).start()
+
+    def chain_finish(bufs, ss, rs):
+        for d in range(1, nf):
+            for i, buf in enumerate(bufs):
+
+                @pl.when(me_f >= d)
+                def _():
+                    g_copy(buf, ss, rs, i, 1, me_f - d).wait_recv()
+
+                    @pl.when(has_right)
+                    def _():
+                        g_copy(buf, ss, rs, i, 1, me_f - d).start()
+
+                @pl.when(me_f + d < nf)
+                def _():
+                    g_copy(buf, ss, rs, i, 0, me_f + d).wait_recv()
+
+                    @pl.when(has_left)
+                    def _():
+                        g_copy(buf, ss, rs, i, 0, me_f + d).start()
+
+    def chain_drain(bufs, ss, rs):
+        for d in range(nf):
+            for i, buf in enumerate(bufs):
+
+                @pl.when(jnp.logical_and(me_f >= d, has_right))
+                def _():
+                    g_copy(buf, ss, rs, i, 1, me_f - d).wait_send()
+
+                @pl.when(jnp.logical_and(me_f + d < nf, has_left))
+                def _():
+                    g_copy(buf, ss, rs, i, 0, me_f + d).wait_send()
+
+    def r_copy(recv, ss, rs, right, o):
+        return fcopy(
+            pp.at[pl.ds(o * rr, rr)], recv.at[right, o], ss.at[o], rs.at[right, o],
+            me_f + 1 if right else me_f - 1,
+        )
+
+    def chain_reduce(recv, ss, rs, total):
+        for j in range(nf - 1):
+            for right, o in ((1, nf - 1 - j), (0, j)):
+                far = me_f < o if right else me_f > o
+                feeds = has_left if right else has_right
+
+                @pl.when(far)
+                def _():
+                    @pl.when(feeds)
+                    def _():
+                        r_copy(recv, ss, rs, right, o).wait_recv()
+                        block = pl.ds(o * rr, rr)
+                        pp[block, :] = (
+                            pp[block, :].astype(F32) + recv[right, o].astype(F32)
+                        ).astype(BF16)
+
+                    r_copy(recv, ss, rs, right, o).start()
+
+        total[...] = pp[own_rows(me_f), :].astype(F32)
+        for right, feeds in ((1, has_left), (0, has_right)):
+
+            @pl.when(feeds)
+            def _():
+                fcopy(
+                    pp.at[own_rows(me_f)], recv.at[right, me_f], ss.at[me_f],
+                    rs.at[right, me_f], me_f - 1 if right else me_f + 1,
+                ).wait_recv()
+                total[...] += recv[right, me_f].astype(F32)
+
+    def reduce_drain(recv, ss, rs):
+        for o in range(nf):
+
+            @pl.when(me_f < o)
+            def _():
+                r_copy(recv, ss, rs, 1, o).wait_send()
+
+            @pl.when(me_f > o)
+            def _():
+                r_copy(recv, ss, rs, 0, o).wait_send()
+
+    def own_rows(p):
+        return pl.ds(pl.multiple_of(p * rr, rr), rr)
+
     def kv_copies(s):
         slot = lax.rem(s, 2)
         return (
@@ -172,19 +274,9 @@
 
     pl.semaphore_wait(barrier, nf - 1 + nh - 1)
 
-    def qkv(d):
-        return [
-            fcopy(buf.at[me_f], buf.at[me_f], qkv_ss.at[i, d], qkv_rs.at[i, d], fpeer(d))
-            for i, buf in enumerate((qall, kall, vall))
-        ]
-
-    for d in range(1, nf):
-        for c in qkv(d):
-            c.start()
+    chain_start((qall, kall, vall), qkv_ss, qkv_rs)
     ow_copy.start()
-    for d in range(1, nf):
-        for c in qkv(d):
-            c.wait_recv()
+    chain_finish((qall, kall, vall), qkv_ss, qkv_rs)
 
     kw = k_ref.shape[1]
 
@@ -312,20 +404,8 @@
 
     lax.fori_loop(0, width // step, project, 0)
 
-    def own_rows(p):
-        return pl.ds(pl.multiple_of(p * rr, rr), rr)
-
-    def pps(d):
-        p = fpeer(d)
-        return fcopy(pp.at[own_rows(p)], pp_recv.at[d - 1], pp_ss.at[d], pp_rs.at[d], p)
-
-    for d in range(1, nf):
-        pps(d).start()
-    for d in range(1, nf):
-        pps(d).wait_recv()
-    x = pp[own_rows(me_f), :].astype(F32)
-    for d in range(1, nf):
-        x = x + pp_recv[d - 1].astype(F32)
+    chain_reduce(pp_recv, pp_ss, pp_rs, resid)
+    x = resid[...]
     x = (resin_ref[...].astype(F32) + x).astype(BF16).astype(F32)
     resid[...] = x
     mine = jnp.sum(x * x, axis=1, keepdims=True)
@@ -344,15 +424,10 @@
     factor = lax.rsqrt(squares / D + 1e-05)
     nrm[me_f] = (resid[...] * factor * gain_ref[...].astype(F32)).astype(BF16)
 
-    def nrms(d):
-        return fcopy(nrm.at[me_f], nrm.at[me_f], nrm_ss.at[d], nrm_rs.at[d], fpeer(d))
-
-    for d in range(1, nf):
-        nrms(d).start()
+    chain_start((nrm,), nrm_ss, nrm_rs)
     acc[...] = jnp.zeros_like(acc)
     dw_copy.wait()
-    for d in range(1, nf):
-        nrms(d).wait_recv()
+    chain_finish((nrm,), nrm_ss, nrm_rs)
 
     qr = total_rows // nh
 
@@ -442,28 +517,17 @@
 
     lax.fori_loop(0, tiles + 4, inner, 0)
 
+    reduce_drain(pp_recv, pp_ss, pp_rs)
+    pp[...] = acc[...].astype(BF16)
+    chain_reduce(dn_recv, dn_ss, dn_rs, low)
+    out_ref[...] = (resid[...] + low[...]).astype(BF16)
+    reduce_drain(dn_recv, dn_ss, dn_rs)
+    chain_drain((qall, kall, vall), qkv_ss, qkv_rs)
+    chain_drain((nrm,), nrm_ss, nrm_rs)
+
     for d in range(1, nf):
-        pps(d).wait_send()
-    pp[...] = acc[...].astype(BF16)
-
-    def dns(d):
-        p = fpeer(d)
-        return fcopy(pp.at[own_rows(p)], dn_recv.at[d - 1], dn_ss.at[d], dn_rs.at[d], p)
-
-    for d in range(1, nf):
-        dns(d).start()
-    for d in range(1, nf):
-        dns(d).wait_recv()
-    y = pp[own_rows(me_f), :].astype(F32)
-    for d in range(1, nf):
-        y = y + dn_recv[d - 1].astype(F32)
-    out_ref[...] = (resid[...] + y).astype(BF16)
-
-    for d in range(1, nf):
-        for c in qkv(d) + nums(d):
+        for c in nums(d):
             c.wait_send()
-        nrms(d).wait_send()
-        dns(d).wait_send()
     for d in range(1, nh):
         sqs(d).wait_send()
     for d in range(1, nx):
@@ -538,7 +602,7 @@
             V((nf - 1, rows, hh), F32),
             V((nh, rows, qw), BF16),
             V((total_rows, width), BF16),
-            V((nf - 1, rr, width), BF16),
+            V((2, nf, rr, width), BF16),
             V((rr, width), F32),
             V((rr, HD), F32),
             V((nh - 1, rr, HD), F32),
@@ -549,20 +613,21 @@
             V((tiles, nx - 1, 2, qr, tile), BF16),
             V((tiles, nh, qr, tile), BF16),
             V((total_rows, width), F32),
-            V((nf - 1, rr, width), BF16),
+            V((2, nf, rr, width), BF16),
+            V((rr, width), F32),
             dma((2, 2)),
             dma((2,)),
             dma((2, SLOTS)),
-            dma((3, nf)), dma((3, nf)),
+            dma((3, 2, nf)), dma((3, nf)),
             dma((2, nf)), dma((2, nf)),
             dma((2 * nx,)), dma((2 * nx,)),
-            dma((nf,)), dma((nf,)),
+            dma((nf,)), dma((2, nf)),
             dma((nh,)), dma((nh,)),
-            dma((nf,)), dma((nf,)),
+            dma((1, 2, nf)), dma((1, nf)),
             dma((tiles,)), dma((tiles,)),
             dma((tiles, nx)), dma((tiles, nx)),
             dma((tiles, 2 * nx)), dma((tiles, 2 * nx)),
-            dma((nf,)), dma((nf,)),
+            dma((nf,)), dma((2, nf)),
         ]
         return pl.pallas_call(
             functools.partial(kernel, (nf, nh, seqs, tile, tiles)),

time: 199 us -> 193 us (0.970)
  the two profiles are of different devices: /device:TPU:24 before, /device:TPU:0 now
where the time goes in v2:
time: 193 us
  Pallas kernels  186 us (96%)
  other arithmetic  3.69 us (2%)
  local copies, waits for them, and re-layouts  3.04 us (2%)
    pallas_call x1, Pallas kernels, shards(): pl.pallas_call(functools.partial(kernel, (nf, nh, seqs, tile, tiles)), ou...  186 us

profile of v2, /device:TPU:0, one launch (start us, length us, event | category | flops | bytes accessed | tf_op | source)
XLA Modules:
  0.0 193.1 jit_solution(180820598504354322)
XLA Ops:
  0.0 0.7 add_convert_fusion
  0.7 0.1 convert_element_type.18
  0.8 1.3 compare_select_fusion.bias_ref
  2.2 1.3 broadcast_in_dim.32.gain_ref
  3.4 0.7 fusion.1.dbias_ref
  4.2 0.2 fusion.2
  4.4 0.7 pad_maximum_fusion
  5.1 186.4 %shard_map.118 = bf16[64,2048]{1,0:T(8,128)(2,1)} custom-call(f32[64,128]{1,0:T(8,128)} %get-tuple-element.8.cos_ref, f32[64,128]{1,0:T(8,128)} %get-tuple-element.9.sin_ref, f32[4,1,512]{2,1,0:T(1,128)} %compare_select_fusion.bias_ref, f32[128,16]{1,0:T(8,128)} %fusion.1.dbias_ref, bf16[64,2048]{1,0:T(8,128)(2,1)} %q_ref.1, bf16[64,256]{1,0:T(8,128)(2,1)} %k_ref.1, ...), custom_call_target="tpu_custom_call" | custom-call | tf_op jit(solution)/shard_map/pallas_call | solution.py:632
  191.5 1.7 copy.14
  (3 shorter events, 0.0 us)
